TPU v7x, 32 devices: a whole 2x2x4 slice. The times are simulated.
32 devices in a mesh: parts: 2 (over x), seq: 16 (over z, y, core).
Axes of the slice: x: 2, y: 2, z: 4, core: 2. Of those that a mesh axis runs over, the one named last changes fastest.
Arguments:
- token_ids: int32 [4, 4], P(None, 'parts'), parts along dimension 1, may hold values from 0 to 76031
- lengths: int32 [4], P('parts'), parts along dimension 0, may hold values from 24576 to 32768, as said below
- embed_table: bfloat16 [76032, 5120], P('seq'), may hold values from -6 to 6
- attn_gain: bfloat16 [5120], replicated, may hold values from 0.25 to 1.75
- w_qkv: bfloat16 [5120, 7168], P('seq'), may hold values from -0.125 to 0.125
- qkv_bias: float32 [7168], replicated, may hold values from -8 to 8
- cache_keys: bfloat16 [4, 32768, 1024], P('parts', 'seq'), parts along dimension 0, may hold values from -300 to 300
- cache_values: bfloat16 [4, 32768, 1024], P('parts', 'seq'), parts along dimension 0, may hold values from -6 to 6
- w_out: bfloat16 [5120, 5120], P(None, 'seq'), may hold values from -0.078125 to 0.078125
- mlp_gain: bfloat16 [5120], replicated, may hold values from 0.25 to 1.75
- w_gate: bfloat16 [5120, 16384], P(None, 'seq'), may hold values from -0.078125 to 0.078125
- w_up: bfloat16 [5120, 16384], P(None, 'seq'), may hold values from -0.078125 to 0.078125
- w_down: bfloat16 [16384, 5120], P('seq'), may hold values from -0.0625 to 0.0625
Outputs:
- attended: bfloat16 [4, 4, 5120], P(None, 'parts'), parts along dimension 1
- layer_out: bfloat16 [4, 4, 5120], P(None, 'parts', 'seq'), parts along dimension 1
There are 2 independent parts, one for each index of `parts`. A program takes and returns all parts, laid end to end along the dimension named above; an argument that names none is the same for every part. Nothing has to cross between parts.
Inputs may be any that keep to these rules, and one draw needn't show every extreme that they name: Cache positions lengths[b] and later are unused; the first prompt fills the whole cache of 32768 positions.
All inputs are finite; a program needn't handle non-finite values.
Results may differ from a plain program's by a relative error of at most 0.017.
The roundings to bfloat16 on the way count: a program that leaves them out, or rounds other values in their place, can miss the bound.
Values may be sent and summed in bfloat16 or wider, within the bound.
A program may use at most 192 MiB of HBM per device.

v0:
```python
import math
import jax
import jax.numpy as jnp
from jax import lax
from jax.sharding import PartitionSpec as P

HEADS = 40
KV_HEADS = 8
HEAD_DIM = 128
NORM_EPS = 1e-06
ROPE_BASE = 1000000.0
MASKED = -1e30


def joined_2(part, axis, combine):
    gathered = jax.tree.map(lambda a: lax.all_gather(a, axis), part)

    def take(source):
        return jax.tree.map(lambda a: lax.dynamic_index_in_dim(a, source, 0, False), gathered)

    return lax.fori_loop(
        1, lax.axis_size(axis), lambda source, state: combine(state, take(source)), take(0)
    )


def rms_normalize(rows, gain):
    mean_square = jnp.mean(rows * rows, axis=-1, keepdims=True)
    return (rows * lax.rsqrt(mean_square + NORM_EPS) * gain.astype(jnp.float32)).astype(
        jnp.bfloat16
    )


def rotate(vectors, positions):
    half_dim = vectors.shape[-1] // 2
    frequency = ROPE_BASE ** (-2.0 * jnp.arange(half_dim, dtype=jnp.float32) / vectors.shape[-1])
    angles = positions.astype(jnp.float32)[..., None, None] * frequency
    cosine = jnp.cos(angles)
    sine_part = jnp.sin(angles)
    widened = vectors.astype(jnp.float32)
    first_half = widened[..., :half_dim]
    second = widened[..., half_dim:]
    joined = jnp.concatenate(
        [first_half * cosine - second * sine_part, second * cosine + first_half * sine_part],
        axis=-1,
    )
    return joined.astype(jnp.bfloat16)


def combine_partials(earlier, latter):
    top_one, total_one, sum_one = earlier
    top_two, total_two, sum_two = latter
    joined_top = jnp.maximum(top_one, top_two)
    scale_one = jnp.exp(top_one - joined_top)
    scale_two = jnp.exp(top_two - joined_top)
    return (
        joined_top,
        total_one * scale_one + total_two * scale_two,
        sum_one * scale_one[..., None] + sum_two * scale_two[..., None],
    )


def body(
    token_ids,
    lengths,
    embed_table,
    attn_gain,
    w_qkv,
    qkv_bias,
    cache_keys,
    cache_values,
    w_out,
    mlp_gain,
    w_gate,
    w_up,
    w_down,
):
    rank = lax.axis_index("seq")
    step_count, batch_count = token_ids.shape
    model_width = embed_table.shape[1]
    vocab_rows = embed_table.shape[0]
    query_width = HEADS * HEAD_DIM
    key_width = KV_HEADS * HEAD_DIM
    group_size = HEADS // KV_HEADS
    local_ids = token_ids - rank * vocab_rows
    inside = (local_ids >= 0) & (local_ids < vocab_rows)
    picked = jnp.take(embed_table, jnp.clip(local_ids, 0, vocab_rows - 1), axis=0)
    partial_rows = jnp.where(inside[..., None], picked.astype(jnp.float32), 0.0)
    stream = lax.psum(partial_rows, "seq")
    normed = rms_normalize(stream, attn_gain).reshape(-1, model_width)
    feature_rows = w_qkv.shape[0]
    normed_local = lax.dynamic_slice_in_dim(normed, rank * feature_rows, feature_rows, 1)
    joint_partial = jnp.dot(normed_local, w_qkv, preferred_element_type=jnp.float32)
    joint_summed = lax.psum(joint_partial, "seq")
    joint = (joint_summed + qkv_bias).astype(jnp.bfloat16).reshape(step_count, batch_count, -1)
    query_part = joint[..., :query_width].reshape(step_count, batch_count, HEADS, HEAD_DIM)
    key_part = joint[..., query_width : query_width + key_width].reshape(
        step_count, batch_count, KV_HEADS, HEAD_DIM
    )
    value_part = joint[..., query_width + key_width :].reshape(
        step_count, batch_count, KV_HEADS, HEAD_DIM
    )
    positions = lengths[None, :] + jnp.arange(step_count, dtype=jnp.int32)[:, None]
    queries = rotate(query_part, positions)
    new_keys = rotate(key_part, positions)
    grouped = queries.reshape(step_count, batch_count, KV_HEADS, group_size, HEAD_DIM)
    score_scale = 1.0 / math.sqrt(HEAD_DIM)
    local_len = cache_keys.shape[1]
    key_blocks = cache_keys.reshape(batch_count, local_len, KV_HEADS, HEAD_DIM)
    value_blocks = cache_values.reshape(batch_count, local_len, KV_HEADS, HEAD_DIM)
    scores = (
        jnp.einsum("sbkgd,bpkd->bkgsp", grouped, key_blocks, preferred_element_type=jnp.float32)
        * score_scale
    )
    places = rank * local_len + jnp.arange(local_len, dtype=jnp.int32)
    valid = (places[None, :] < lengths[:, None])[:, None, None, None, :]
    masked = jnp.where(valid, scores, MASKED)
    local_top = jnp.max(masked, axis=-1)
    weights = jnp.where(valid, jnp.exp(masked - local_top[..., None]), 0.0)
    local_total = jnp.sum(weights, axis=-1)
    local_sum = jnp.einsum(
        "bkgsp,bpkd->bkgsd",
        weights.astype(jnp.bfloat16),
        value_blocks,
        preferred_element_type=jnp.float32,
    )
    merged_top, merged_total, merged_sum = joined_2(
        (local_top, local_total, local_sum), "seq", combine_partials
    )
    new_scores = (
        jnp.einsum("sbkgd,tbkd->bkgst", grouped, new_keys, preferred_element_type=jnp.float32)
        * score_scale
    )
    step_index = jnp.arange(step_count, dtype=jnp.int32)
    causal = step_index[:, None] >= step_index[None, :]
    new_masked = jnp.where(causal, new_scores, MASKED)
    final_top = jnp.maximum(merged_top, jnp.max(new_masked, axis=-1))
    rescale = jnp.exp(merged_top - final_top)
    new_weights = jnp.where(causal, jnp.exp(new_masked - final_top[..., None]), 0.0)
    final_total = merged_total * rescale + jnp.sum(new_weights, axis=-1)
    final_sum = merged_sum * rescale[..., None] + jnp.einsum(
        "bkgst,tbkd->bkgsd",
        new_weights.astype(jnp.bfloat16),
        value_part,
        preferred_element_type=jnp.float32,
    )
    attended = jnp.transpose(final_sum / final_total[..., None], (3, 0, 1, 2, 4))
    attended = attended.reshape(step_count, batch_count, query_width).astype(jnp.bfloat16)
    shard_cols = w_out.shape[1]
    projected = jnp.dot(
        attended.reshape(-1, query_width), w_out, preferred_element_type=jnp.float32
    )
    stream_shard = lax.dynamic_slice_in_dim(stream, rank * shard_cols, shard_cols, 2)
    mid_shard = stream_shard + projected.reshape(step_count, batch_count, shard_cols)
    squares = lax.psum(jnp.sum(mid_shard * mid_shard, axis=-1), "seq")
    row_scale = lax.rsqrt(squares / model_width + NORM_EPS)
    gain_shard = lax.dynamic_slice_in_dim(mlp_gain, rank * shard_cols, shard_cols, 0).astype(
        jnp.float32
    )
    normed_shard = (mid_shard * row_scale[..., None] * gain_shard).astype(jnp.bfloat16)
    normed_mid = lax.all_gather(normed_shard, "seq", axis=2, tiled=True)
    flat_rows = normed_mid.reshape(-1, model_width)
    gate = jnp.dot(flat_rows, w_gate, preferred_element_type=jnp.float32)
    upper = jnp.dot(flat_rows, w_up, preferred_element_type=jnp.float32)
    hidden = (jax.nn.silu(gate) * upper).astype(jnp.bfloat16)
    down_terms = jnp.dot(hidden, w_down, preferred_element_type=jnp.float32).reshape(
        step_count, batch_count, model_width
    )
    summed = lax.psum_scatter(down_terms, "seq", scatter_dimension=2, tiled=True)
    layer_out = (mid_shard + summed).astype(jnp.bfloat16)
    return (attended, layer_out)


def solution(mesh):
    return jax.shard_map(
        body,
        mesh=mesh,
        in_specs=(
            P(None, "parts"),
            P("parts"),
            P("seq", None),
            P(),
            P("seq", None),
            P(),
            P("parts", "seq", None),
            P("parts", "seq", None),
            P(None, "seq"),
            P(),
            P(None, "seq"),
            P(None, "seq"),
            P("seq", None),
        ),
        out_specs=(P(None, "parts", None), P(None, "parts", "seq")),
        check_vma=False,
    )
```

profile of v0, /device:TPU:0, one launch (start us, length us, event | category | flops | bytes accessed | tf_op | source)
XLA Modules:
  0.0 495.7 jit_solution(8823497209833906688)
XLA Ops:
  8.3 1.9 gather_fusion
  13.4 8.8 %copy.106 = bf16[512,8,8,128]{3,2,1,0:T(8,128)(2,1)} copy(bf16[512,8,8,128]{3,1,2,0:T(8,128)(2,1)} %bitcast.100) | data formatting | bytes 16777216
  22.2 7.1 %bitcast_bitcast_fusion.1 = bf16[2,2048,8,128,1]{3,2,1,0,4:T(8,128)(2,1)} fusion(bf16[2,2048,8,128]{3,2,1,0:T(8,128)(2,1)} %bitcast.97), kind=kLoop, calls=%fused_computation.12 | loop fusion | bytes 16777216 | tf_op jit(solution)/shard_map/reshape | solution.py:108
  29.3 8.8 %copy.107 = bf16[512,8,8,128]{3,2,1,0:T(8,128)(2,1)} copy(bf16[512,8,8,128]{3,1,2,0:T(8,128)(2,1)} %bitcast.101) | data formatting | bytes 16777216
  38.1 7.0 %bitcast_bitcast_fusion = bf16[2,2048,8,128,1]{3,2,1,0,4:T(8,128)(2,1)} fusion(bf16[2,2048,8,128]{3,2,1,0:T(8,128)(2,1)} %bitcast.98), kind=kLoop, calls=%fused_computation.11 | loop fusion | bytes 16777216 | tf_op jit(solution)/shard_map/reshape | solution.py:109
  45.2 57.9 %all-reduce.3.cloned.1.call-done = f32[4,2,5120]{2,1,0:T(2,128)} async-done(((f32[4,2,5120]{2,1,0:T(2,128)}), f32[4,2,5120]{2,1,0:T(2,128)}) %all-reduce.3.cloned.1.call-update) | async-done | bytes 163856 | tf_op jit(solution)/shard_map/psum | solution.py:88
  105.3 3.7 fusion.47
  109.4 90.0 %all-reduce.5.cloned.1.call-done = f32[8,7168]{1,0:T(8,128)} async-done(((f32[8,7168]{1,0:T(8,128)}), f32[8,7168]{1,0:T(8,128)}) %all-reduce.5.cloned.1.call-update) | async-done | bytes 229392 | tf_op jit(solution)/shard_map/psum | solution.py:93
  201.2 6.3 %bitcast_reduce_fusion = (f32[2,8,5,4]{2,3,1,0:T(4,128)S(1)}, f32[2,8,4,5,2048]{4,3,2,1,0:T(8,128)S(1)}) fusion(pred[2,2048]{1,0:T(4,128)(4,1)S(1)} %broadcast_compare_fusion, bf16[2,2048,8,128,1]{3,2,1,0,4:T(8,128)(2,1)} %bitcast_bitcast_fusion.1, bf16[4,2,8,5,64]{4,3,0,2,1:T(8,128)(2,1)S(1)} %copy.69, bf16[4,2,8,5,64]{4,3,0,2,1:T(8,128)(2,1)S(1)} %copy.68), kind=kOutput, calls=%fused_computation.18 | convolution fusion | flops 169901760 | bytes 11097344 | tf_op jit(solution)/shard_map/sbkgd,bpkd->bkgsp/dot_general | solution.py:111
  207.6 3.1 fusion.4
  212.5 3.6 fusion.13
  216.2 23.1 %all-gather.1 = f32[32,8,5,4]{1,3,2,0:T(4,128)S(1)} all-gather(f32[2,8,5,4]{1,3,2,0:T(4,128)S(1)} %copy.72), channel_id=3, replica_groups=mesh['parts'=2,'seq'=16] {'seq'}, dimensions={0}, use_global_device_ids=true | all-gather | bytes 21760 | tf_op jit(solution)/shard_map/all_gather | solution.py:16
  240.1 19.3 %all-gather = f32[32,8,5,4]{1,3,2,0:T(4,128)S(1)} all-gather(f32[2,8,5,4]{1,3,2,0:T(4,128)S(1)} %copy.71), channel_id=2, replica_groups=mesh['parts'=2,'seq'=16] {'seq'}, dimensions={0}, use_global_device_ids=true | all-gather | bytes 21760 | tf_op jit(solution)/shard_map/all_gather | solution.py:16
  261.1 2.3 fusion.60
  265.1 57.2 %while.19 = (s32[]{:T(128)}, f32[2,8,5,4]{1,3,2,0:T(4,128)S(1)}, f32[2,8,5,4]{1,3,2,0:T(4,128)S(1)}, f32[2,8,5,4,128]{4,3,2,1,0:T(4,128)}, f32[16,2,8,5,4]{2,4,3...) while((s32[]{:T(128)}, f32[2,8,5,4]{1,3,2,0:T(4,128)S(1)}, ...), condition=%wide.region_6.7_spmd, body=%wide.region_5.6_spmd.sunk | while | flops 124805 | bytes 837271 | solution.py:21
  327.0 30.7 %psum.23 = f32[4,2]{1,0:T(4,128)S(1)} all-reduce(f32[4,2]{1,0:T(4,128)S(1)} %get-tuple-element.245), channel_id=1, replica_groups=mesh['parts'=2,'seq'=16] {'seq'}, use_global_device_ids=true, to_apply=%region_10.11 | all-reduce | flops 8 | bytes 64 | tf_op jit(solution)/shard_map/psum | solution.py:154
  357.9 33.2 %all_gather.27 = bf16[4,2,5120]{0,1,2:T(2,128)(2,1)} all-gather(bf16[4,2,320]{0,1,2:T(2,128)(2,1)S(1)} %copy.85), channel_id=1, replica_groups=mesh['parts'=2,'seq'=16] {'seq'}, dimensions={2}, use_global_device_ids=true | all-gather | bytes 87040 | tf_op jit(solution)/shard_map/all_gather | solution.py:160
  391.2 5.2 %copy.86 = bf16[4,2,5120]{2,1,0:T(2,128)(2,1)S(1)} copy(bf16[4,2,5120]{0,1,2:T(2,128)(2,1)} %all_gather.27) | data formatting | bytes 163840 | tf_op jit(solution)/shard_map/all_gather | solution.py:160
  396.5 5.4 %fusion.61 = f32[8,1024]{1,0:T(8,128)S(1)} fusion(bf16[8,5120]{1,0:T(8,128)(2,1)S(1)} %reshape.133, bf16[5120,1024]{1,0:T(8,128)(2,1)} %param.25), kind=kOutput, calls=%fused_computation.105 | convolution fusion | flops 83886080 | bytes 10600448 | tf_op jit(solution)/shard_map/dot_general | solution.py:162
  401.9 9.8 %fusion.30 = f32[8,5120]{1,0:T(8,128)S(1)} fusion(bf16[1024,5120]{1,0:T(8,128)(2,1)} %param.27, bf16[8,5120]{1,0:T(8,128)(2,1)S(1)} %reshape.133, bf16[5120,1024]{1,0:T(8,128)(2,1)} %param.26, f32[8,1024]{1,0:T(8,128)S(1)} %fusion.61), kind=kOutput, calls=%fused_computation.42 | convolution fusion | flops 167821312 | bytes 21250048 | tf_op jit(solution)/shard_map/dot_general | solution.py:165
  412.5 5.9 %copy.99 = f32[4,2,5120]{0,1,2:T(2,128)} copy(f32[4,2,5120]{2,1,0:T(2,128)} %reshape.134) | data formatting | bytes 327680
  418.4 6.0 %reshape.161 = f32[5120,8]{1,0:T(8,128)} reshape(f32[5120,2,4]{2,1,0:T(2,128)} %bitcast.99) | data formatting | bytes 327680
  424.4 61.2 %reduce-scatter.4.cloned.1.call-done = f32[320,8]{1,0:T(8,128)} async-done(((f32[5120,8]{1,0:T(8,128)}), f32[320,8]{1,0:T(8,128)}) %reduce-scatter.4.cloned.1.call-update) | async-done | bytes 10256
  485.5 1.9 reshape.162
  (165 shorter events, 79.1 us)
Async XLA Ops:
  7.2 317.9 %copy-start = (bf16[5120,320]{0,1:T(8,128)(2,1)S(1)}, bf16[5120,320]{0,1:T(8,128)(2,1)}, u32[]{:S(2)}) copy-start(bf16[5120,320]{0,1:T(8,128)(2,1)} %param.23) | copy-start | bytes 9830404
  7.2 95.9 %all-reduce.3.cloned.1.call-start = ((), (), s32[]{:S(2)}) async-start(), calls=%async_computation.1 | async-start | bytes 327680 | tf_op jit(solution)/shard_map/psum | solution.py:88
  11.2 188.2 %all-reduce.5.cloned.1.call-start = ((), (), s32[]{:S(2)}) async-start(), calls=%async_computation.2 | async-start | bytes 458752 | tf_op jit(solution)/shard_map/psum | solution.py:93
  45.2 154.3 %copy-start.9 = (f32[7168]{0:T(1024)S(1)}, f32[7168]{0:T(1024)}, u32[]{:S(2)}) copy-start(f32[7168]{0:T(1024)} %param.20) | copy-start | bytes 86020
  109.1 154.3 %all-gather.5.cloned.1.call-start = ((), (), s32[]{:S(2)}) async-start(), calls=%async_computation.3 | async-start | bytes 2785280 | tf_op jit(solution)/shard_map/all_gather | solution.py:16
  200.4 0.7 copy-start.5
  201.1 6.5 %slice-start = ((s8[8388608]{0:T(1024)(128)(4,1)}), s8[4194304]{0:T(1024)(128)(4,1)S(1)}, s32[]{:S(2)}) async-start(s8[8388608]{0:T(1024)(128)(4,1)} %bitcast.102), calls=%async_computation.5 | async-start | bytes 8388608
  201.2 6.4 %copy-start.4 = (bf16[4,2,8,5,64]{4,3,0,2,1:T(8,128)(2,1)}, bf16[4,2,8,5,64]{4,3,0,2,1:T(8,128)(2,1)S(1)}, u32[]{:S(2)}) copy-start(bf16[4,2,8,5,64]{4,3,0,2,1:T(8,128)(2,1)S(1)} %copy.69) | copy-start | bytes 122884
  201.2 6.4 %slice-start.1 = ((s8[8388608]{0:T(1024)(128)(4,1)}), s8[4194304]{0:T(1024)(128)(4,1)S(1)}, s32[]{:S(2)}) async-start(s8[8388608]{0:T(1024)(128)(4,1)} %bitcast.102), calls=%async_computation.6 | async-start | bytes 8388608
  207.5 3.2 copy-start.1
  211.5 274.0 %reduce-scatter.4.cloned.1.call-start = ((), (), s32[]{:S(2)}) async-start(), calls=%async_computation.4 | async-start | bytes 2785280
  239.3 0.7 copy-start.2
  259.4 0.7 copy-start.3
  325.1 32.6 %copy-start.6 = (bf16[4,2,5120]{2,1,0:T(2,128)(2,1)}, bf16[4,2,5120]{2,1,0:T(2,128)(2,1)S(1)}, u32[]{:S(2)}) copy-start(bf16[4,2,5120]{2,1,0:T(2,128)(2,1)S(1)} %convert_element_type.77) | copy-start | bytes 245764
  327.0 30.7 %copy-start.7 = (f32[4,2,320]{2,1,0:T(2,128)}, f32[4,2,320]{2,1,0:T(2,128)S(1)}, u32[]{:S(2)}) copy-start(f32[4,2,320]{2,1,0:T(2,128)S(1)} %get-tuple-element.246) | copy-start | bytes 30724
  418.4 70.1 %copy-start.8 = (f32[4,2,320]{2,1,0:T(2,128)S(1)}, f32[4,2,320]{2,1,0:T(2,128)}, u32[]{:S(2)}) copy-start(f32[4,2,320]{2,1,0:T(2,128)} %copy-done.7) | copy-start | bytes 30724
Sparse Core Ops, SparseCore 0:
  11.4 91.6 all-reduce.2
  109.2 90.1 all-reduce.4
  211.6 46.0 all-gather.4
  424.5 61.0 reduce-scatter.3
where the time goes:
time: 499 us; the launch traced here: 496 us
  waiting for transfers between devices  209 us (42%)
  blocking collectives  106 us (21%)
  local copies, waits for them, and re-layouts  78.3 us (16%)
  other arithmetic  53.3 us (11%)
  matrix products  34 us (7%)
  between operations  14.1 us (3%)
    psum x1, waiting for transfers between devices, body(): joint_summed = lax.psum(joint_partial, 'seq')  90 us
    unnamed x5, waiting for transfers between devices  61.2 us
    psum x1, waiting for transfers between devices, body(): stream = lax.psum(partial_rows, 'seq')  57.9 us
    all_gather x2, blocking collectives, joined_2(): gathered = jax.tree.map(lambda a: lax.all_gather(a, axis), part)  42.5 us
    all_gather x1, blocking collectives, body(): normed_mid = lax.all_gather(normed_shard, 'seq', axis=2, tiled=True)  33.2 us
    unnamed x29, local copies, waits for them, and re-layouts  33.1 us
    psum x1, blocking collectives, body(): squares = lax.psum(jnp.sum(mid_shard * mid_shard, axis=-1), 'seq')  30.7 us
    add x15, other arithmetic, combine_partials(): sum_one * scale_one[..., None] + sum_two * scale_two[..., None]  27.3 us
  transfers between devices with their start and end apart: 4, of which 3 were waited for; matrix products, arithmetic and copies ran while one was open for 8% of the time, Pallas kernels for 0%

commit v1 on v0

--- a/solution.py
+++ b/solution.py
@@ -85,7 +85,7 @@
     inside = (local_ids >= 0) & (local_ids < vocab_rows)
     picked = jnp.take(embed_table, jnp.clip(local_ids, 0, vocab_rows - 1), axis=0)
     partial_rows = jnp.where(inside[..., None], picked.astype(jnp.float32), 0.0)
-    stream = lax.psum(partial_rows, "seq")
+    stream = jnp.sum(jax.lax.all_gather(partial_rows, "seq"), 0)
     normed = rms_normalize(stream, attn_gain).reshape(-1, model_width)
     feature_rows = w_qkv.shape[0]
     normed_local = lax.dynamic_slice_in_dim(normed, rank * feature_rows, feature_rows, 1)

time: 499 us -> 452 us (0.906)
  waiting for transfers between devices: 209 us -> 164 us
    psum x1 -> x0, waiting for transfers between devices: 57.9 us -> none  [body(): stream = lax.psum(partial_rows, 'seq')]
    all_gather x0 -> x1, waiting for transfers between devices: none -> 14.6 us  [body(): stream = jnp.sum(jax.lax.all_gather(partial_rows, 'seq'), 0)]
    unnamed x29 -> x35, local copies, waits for them, and re-layouts: 33.1 us -> 35.7 us
where the time goes in v1:
time: 452 us; the launch traced here: 450 us
  waiting for transfers between devices  164 us (36%)
  blocking collectives  106 us (23%)
  local copies, waits for them, and re-layouts  79.5 us (18%)
  other arithmetic  51.4 us (11%)
  matrix products  34 us (8%)
  between operations  14.1 us (3%)
    psum x1, waiting for transfers between devices, body(): joint_summed = lax.psum(joint_partial, 'seq')  87.9 us
    unnamed x5, waiting for transfers between devices  61.2 us
    all_gather x2, blocking collectives, joined_2(): gathered = jax.tree.map(lambda a: lax.all_gather(a, axis), part)  42.7 us
    unnamed x35, local copies, waits for them, and re-layouts  35.7 us
    all_gather x1, blocking collectives, body(): normed_mid = lax.all_gather(normed_shard, 'seq', axis=2, tiled=True)  33.6 us
    psum x1, blocking collectives, body(): squares = lax.psum(jnp.sum(mid_shard * mid_shard, axis=-1), 'seq')  30.2 us
    add x15, other arithmetic, combine_partials(): sum_one * scale_one[..., None] + sum_two * scale_two[..., None]  27.3 us
    dynamic_slice x18, local copies, waits for them, and re-layouts, take(): lax.dynamic_index_in_dim(a, source, 0, False)  14.9 us
  transfers between devices with their start and end apart: 4, of which 3 were waited for; matrix products, arithmetic and copies ran while one was open for 8% of the time, Pallas kernels for 0%

profile of v1, /device:TPU:0, one launch (start us, length us, event | category | flops | bytes accessed | tf_op | source)
XLA Modules:
  0.0 449.6 jit_solution(5400480129607817109)
XLA Ops:
  11.0 8.8 %copy.152 = bf16[512,8,8,128]{3,2,1,0:T(8,128)(2,1)} copy(bf16[512,8,8,128]{3,1,2,0:T(8,128)(2,1)} %bitcast.100) | data formatting | bytes 16777216
  19.8 9.0 %copy.153 = bf16[512,8,8,128]{3,2,1,0:T(8,128)(2,1)} copy(bf16[512,8,8,128]{3,1,2,0:T(8,128)(2,1)} %bitcast.101) | data formatting | bytes 16777216
  29.7 7.5 %bitcast_bitcast_fusion.1 = bf16[2,2048,8,128,1]{3,2,1,0,4:T(8,128)(2,1)} fusion(bf16[2,2048,8,128]{3,2,1,0:T(8,128)(2,1)} %bitcast.98), kind=kLoop, calls=%fused_computation.12 | loop fusion | bytes 16777216 | tf_op jit(solution)/shard_map/reshape | solution.py:108
  38.7 3.6 bitcast_bitcast_fusion
  42.2 14.6 %all-gather.6.cloned.1.call-done = f32[16,4,2,5120]{3,1,2,0:T(4,128)} async-done(((f32[1,4,2,5120]{3,1,2,0:T(4,128)}), f32[16,4,2,5120]{3,1,2,0:T(4,128)}) %all-gather.6.cloned.1.call-update) | async-done | bytes 2621456 | tf_op jit(solution)/shard_map/all_gather | solution.py:88
  56.8 2.2 reduce_sum.47
  61.2 3.7 fusion.49
  65.3 87.9 %all-reduce.2.cloned.1.call-done = f32[8,7168]{1,0:T(8,128)} async-done(((f32[8,7168]{1,0:T(8,128)}), f32[8,7168]{1,0:T(8,128)}) %all-reduce.2.cloned.1.call-update) | async-done | bytes 229392 | tf_op jit(solution)/shard_map/psum | solution.py:93
  154.9 6.3 %bitcast_reduce_fusion = (f32[2,8,5,4]{2,3,1,0:T(4,128)S(1)}, f32[2,8,4,5,2048]{4,3,2,1,0:T(8,128)S(1)}) fusion(pred[2,2048]{1,0:T(4,128)(4,1)S(1)} %broadcast_compare_fusion, bf16[2,2048,8,128,1]{3,2,1,0,4:T(8,128)(2,1)} %bitcast_bitcast_fusion.1, bf16[4,2,8,5,64]{4,3,0,2,1:T(8,128)(2,1)S(1)} %copy.111, bf16[4,2,8,5,64]{4,3,0,2,1:T(8,128)(2,1)S(1)} %copy.110), kind=kOutput, calls=%fused_computation.18 | convolution fusion | flops 169901760 | bytes 11097344 | tf_op jit(solution)/shard_map/sbkgd,bpkd->bkgsp/dot_general | solution.py:111
  161.3 3.1 fusion.4
  165.5 3.6 fusion.13
  169.2 22.9 %all-gather.1 = f32[32,8,5,4]{1,3,2,0:T(4,128)S(1)} all-gather(f32[2,8,5,4]{1,3,2,0:T(4,128)S(1)} %copy.114), channel_id=3, replica_groups=mesh['parts'=2,'seq'=16] {'seq'}, dimensions={0}, use_global_device_ids=true | all-gather | bytes 21760 | tf_op jit(solution)/shard_map/all_gather | solution.py:16
  192.8 19.8 %all-gather = f32[32,8,5,4]{1,3,2,0:T(4,128)S(1)} all-gather(f32[2,8,5,4]{1,3,2,0:T(4,128)S(1)} %copy.113), channel_id=2, replica_groups=mesh['parts'=2,'seq'=16] {'seq'}, dimensions={0}, use_global_device_ids=true | all-gather | bytes 21760 | tf_op jit(solution)/shard_map/all_gather | solution.py:16
  214.3 2.3 fusion.64
  218.3 57.2 %while.19 = (s32[]{:T(128)}, f32[2,8,5,4]{1,3,2,0:T(4,128)S(1)}, f32[2,8,5,4]{1,3,2,0:T(4,128)S(1)}, f32[2,8,5,4,128]{4,3,2,1,0:T(4,128)}, f32[16,2,8,5,4]{2,4,3...) while((s32[]{:T(128)}, f32[2,8,5,4]{1,3,2,0:T(4,128)S(1)}, ...), condition=%wide.region_6.7_spmd, body=%wide.region_5.6_spmd.sunk | while | flops 124805 | bytes 837271 | solution.py:21
  281.0 30.2 %psum.15 = f32[4,2]{0,1:T(2,128)S(1)} all-reduce(f32[4,2]{0,1:T(2,128)S(1)} %copy.149), channel_id=1, replica_groups=mesh['parts'=2,'seq'=16] {'seq'}, use_global_device_ids=true, to_apply=%region_10.11 | all-reduce | flops 8 | bytes 64 | tf_op jit(solution)/shard_map/psum | solution.py:154
  311.5 33.6 %all_gather.32 = bf16[4,2,5120]{0,1,2:T(2,128)(2,1)} all-gather(bf16[4,2,320]{0,1,2:T(2,128)(2,1)S(1)} %copy.129), channel_id=1, replica_groups=mesh['parts'=2,'seq'=16] {'seq'}, dimensions={2}, use_global_device_ids=true | all-gather | bytes 87040 | tf_op jit(solution)/shard_map/all_gather | solution.py:160
  345.2 5.2 %copy.130 = bf16[4,2,5120]{2,1,0:T(2,128)(2,1)S(1)} copy(bf16[4,2,5120]{0,1,2:T(2,128)(2,1)} %all_gather.32) | data formatting | bytes 163840 | tf_op jit(solution)/shard_map/all_gather | solution.py:160
  350.4 5.4 %fusion.65 = f32[8,1024]{1,0:T(8,128)S(1)} fusion(bf16[8,5120]{1,0:T(8,128)(2,1)S(1)} %reshape.152, bf16[5120,1024]{1,0:T(8,128)(2,1)} %param.25), kind=kOutput, calls=%fused_computation.108 | convolution fusion | flops 83886080 | bytes 10600448 | tf_op jit(solution)/shard_map/dot_general | solution.py:162
  355.9 9.8 %fusion.30 = f32[8,5120]{1,0:T(8,128)S(1)} fusion(bf16[1024,5120]{1,0:T(8,128)(2,1)} %param.27, bf16[8,5120]{1,0:T(8,128)(2,1)S(1)} %reshape.152, bf16[5120,1024]{1,0:T(8,128)(2,1)} %param.26, f32[8,1024]{1,0:T(8,128)S(1)} %fusion.65), kind=kOutput, calls=%fused_computation.42 | convolution fusion | flops 167821312 | bytes 21250048 | tf_op jit(solution)/shard_map/dot_general | solution.py:165
  366.4 5.9 %copy.143 = f32[4,2,5120]{0,1,2:T(2,128)} copy(f32[4,2,5120]{2,1,0:T(2,128)} %reshape.153) | data formatting | bytes 327680
  372.4 6.0 %reshape.181 = f32[5120,8]{1,0:T(8,128)} reshape(f32[5120,2,4]{2,1,0:T(2,128)} %bitcast.99) | data formatting | bytes 327680
  378.4 61.1 %reduce-scatter.4.cloned.1.call-done = f32[320,8]{1,0:T(8,128)} async-done(((f32[5120,8]{1,0:T(8,128)}), f32[320,8]{1,0:T(8,128)}) %reduce-scatter.4.cloned.1.call-update) | async-done | bytes 10256
  439.5 1.9 reshape.182
  (172 shorter events, 81.0 us)
Async XLA Ops:
  7.2 271.1 %copy-start = (bf16[5120,320]{0,1:T(8,128)(2,1)S(1)}, bf16[5120,320]{0,1:T(8,128)(2,1)}, u32[]{:S(2)}) copy-start(bf16[5120,320]{0,1:T(8,128)(2,1)} %param.23) | copy-start | bytes 9830404
  7.2 49.6 %all-gather.6.cloned.1.call-start = ((), (), s32[]{:S(2)}) async-start(), calls=%async_computation.1 | async-start | bytes 2785280 | tf_op jit(solution)/shard_map/all_gather | solution.py:88
  11.0 142.2 %all-reduce.2.cloned.1.call-start = ((), (), s32[]{:S(2)}) async-start(), calls=%async_computation.2 | async-start | bytes 458752 | tf_op jit(solution)/shard_map/psum | solution.py:93
  19.8 9.7 %copy-start.11 = (s32[2]{0:T(128)S(1)}, s32[2]{0:T(128)}, u32[]{:S(2)}) copy-start(s32[2]{0:T(128)} %param.16) | copy-start | bytes 28
  29.7 9.0 %copy-start.1 = (bf16[512,8,8,128]{3,2,1,0:T(8,128)(2,1)S(1)}, bf16[512,8,8,128]{3,2,1,0:T(8,128)(2,1)}, u32[]{:S(2)}) copy-start(bf16[512,8,8,128]{3,2,1,0:T(8,128)(2,1)} %copy.153) | copy-start | bytes 25165828
  42.2 111.0 %copy-start.10 = (f32[7168]{0:T(1024)S(1)}, f32[7168]{0:T(1024)}, u32[]{:S(2)}) copy-start(f32[7168]{0:T(1024)} %param.20) | copy-start | bytes 86020
  64.9 151.7 %all-gather.8.cloned.1.call-start = ((), (), s32[]{:S(2)}) async-start(), calls=%async_computation.3 | async-start | bytes 2785280 | tf_op jit(solution)/shard_map/all_gather | solution.py:16
  154.2 0.7 copy-start.6
  154.9 6.5 %slice-start = ((s8[8388608]{0:T(1024)(128)(4,1)}), s8[4194304]{0:T(1024)(128)(4,1)S(1)}, s32[]{:S(2)}) async-start(s8[8388608]{0:T(1024)(128)(4,1)} %bitcast.102), calls=%async_computation.5 | async-start | bytes 8388608
  154.9 6.4 %copy-start.5 = (bf16[4,2,8,5,64]{4,3,0,2,1:T(8,128)(2,1)}, bf16[4,2,8,5,64]{4,3,0,2,1:T(8,128)(2,1)S(1)}, u32[]{:S(2)}) copy-start(bf16[4,2,8,5,64]{4,3,0,2,1:T(8,128)(2,1)S(1)} %copy.111) | copy-start | bytes 122884
  154.9 6.4 %slice-start.1 = ((s8[8388608]{0:T(1024)(128)(4,1)}), s8[4194304]{0:T(1024)(128)(4,1)S(1)}, s32[]{:S(2)}) async-start(s8[8388608]{0:T(1024)(128)(4,1)} %bitcast.102), calls=%async_computation.6 | async-start | bytes 8388608
  161.3 3.2 copy-start.2
  165.3 274.2 %reduce-scatter.4.cloned.1.call-start = ((), (), s32[]{:S(2)}) async-start(), calls=%async_computation.4 | async-start | bytes 2785280
  192.1 0.7 copy-start.3
  212.6 0.7 copy-start.4
  278.3 33.0 %copy-start.7 = (bf16[4,2,5120]{2,1,0:T(2,128)(2,1)}, bf16[4,2,5120]{2,1,0:T(2,128)(2,1)S(1)}, u32[]{:S(2)}) copy-start(bf16[4,2,5120]{2,1,0:T(2,128)(2,1)S(1)} %convert_element_type.85) | copy-start | bytes 245764
  280.1 31.1 %copy-start.8 = (f32[4,2,320]{2,1,0:T(2,128)}, f32[4,2,320]{2,1,0:T(2,128)S(1)}, u32[]{:S(2)}) copy-start(f32[4,2,320]{2,1,0:T(2,128)S(1)} %get-tuple-element.253) | copy-start | bytes 30724
  372.4 70.1 %copy-start.9 = (f32[4,2,320]{2,1,0:T(2,128)S(1)}, f32[4,2,320]{2,1,0:T(2,128)}, u32[]{:S(2)}) copy-start(f32[4,2,320]{2,1,0:T(2,128)} %copy-done.8) | copy-start | bytes 30724
Sparse Core Ops, SparseCore 0:
  11.1 45.6 all-gather.5
  65.1 88.0 all-reduce.1
  165.4 45.4 all-gather.7
  378.5 60.9 reduce-scatter.3
